TPU v7x, 32 devices: a whole 2x2x4 slice. The times are simulated.
32 devices in a mesh: wide: 8 (over z, x), narrow: 4 (over y, core).
Axes of the slice: x: 2, y: 2, z: 4, core: 2. Of those that a mesh axis runs over, the one named last changes fastest.
Arguments:
- old_basis: float32 [16, 2048, 512], P(None, ('wide', 'narrow')), may hold values from -6 to 6
- restart_coeffs: float32 [16], replicated, may hold values from -1 to 1
- geometry: float32 [4, 2048, 512], P(None, ('wide', 'narrow')), may hold values from 0.01 to 18, as said below
- orientation: int32 [6, 2048], P(None, ('wide', 'narrow')), may hold values from 0 to 7
Outputs:
- new_basis: float32 [2, 2048, 512], P(None, ('wide', 'narrow'))
- hessenberg: float32 [2, 18], replicated
Inputs may be any that keep to these rules, and one draw needn't show every extreme that they name: `geometry`: every entry is positive.
All inputs are finite; a program needn't handle non-finite values.
Results may differ from a plain program's by a relative error of at most 0.0003.
Values sent between devices are 32-bit elements; how exact they have to be, the bound alone decides.
A program may use at most 64 MiB of HBM per device.

v0:
```python
import jax
import jax.numpy as jnp
import numpy as np
from jax import lax
from jax.sharding import PartitionSpec as P

NP = 8
EX = 4
EY = 4
EZ = 4


highest = lax.Precision.HIGHEST
epsilon = 1e-06


def padded_2(block, sides, width):
    for axis, dim in sides:
        count = lax.axis_size(axis)
        forward = [(i, i + 1) for i in range(count - 1)]
        backward = [(target, source) for source, target in forward]
        low = lax.ppermute(
            lax.slice_in_dim(block, block.shape[dim] - width, None, axis=dim), axis, forward
        )
        high = lax.ppermute(lax.slice_in_dim(block, 0, width, axis=dim), axis, backward)
        block = jnp.concatenate([low, block, high], axis=dim)
    return block


def legendre_columns(nodes, degree):
    columns = [nodes * 0.0 + 1.0, nodes * 1.0]
    for order in range(2, degree + 1):
        columns.append(
            ((2 * order - 1) * nodes * columns[order - 1] - (order - 1) * columns[order - 2])
            / order
        )
    return columns


def gll_derivative(extent):
    degree = extent - 1
    nodes = np.cos(np.pi * np.arange(extent) / degree)
    for sweep in range(100):
        columns = legendre_columns(nodes, degree)
        nodes = nodes - (nodes * columns[degree] - columns[degree - 1]) / (extent * columns[degree])
    gll_nodes = nodes[::-1] * 1.0
    values = legendre_columns(gll_nodes, degree)[degree]
    matrix = np.zeros((extent, extent))
    for row_idx in range(extent):
        for col_idx in range(extent):
            if row_idx != col_idx:
                matrix[row_idx, col_idx] = values[row_idx] / (
                    values[col_idx] * (gll_nodes[row_idx] - gll_nodes[col_idx])
                )
    matrix[0, 0] = -degree * (degree + 1) / 4.0
    matrix[extent - 1, extent - 1] = degree * (degree + 1) / 4.0
    return matrix


def face_point(face_kind, row_pos, col_pos, extent):
    far_end = extent - 1
    if face_kind == 0:
        return (0, row_pos, col_pos)
    if face_kind == 1:
        return (far_end, row_pos, col_pos)
    if face_kind == 2:
        return (row_pos, 0, col_pos)
    if face_kind == 3:
        return (row_pos, far_end, col_pos)
    if face_kind == 4:
        return (row_pos, col_pos, 0)
    return (row_pos, col_pos, far_end)


def spectral_tables(extent):
    matrix = gll_derivative(extent)
    identity = np.eye(extent)
    along_x = np.kron(np.kron(matrix, identity), identity)
    along_y = np.kron(np.kron(identity, matrix), identity)
    along_z = np.kron(np.kron(identity, identity), matrix)
    forward = np.concatenate([along_x.T, along_y.T, along_z.T], axis=1)
    backward = np.concatenate([along_x, along_y, along_z], axis=0)
    square = extent * extent
    select = np.zeros((extent**3, 6 * square))
    rotations = np.zeros((square, 8 * square))
    for face_kind in range(6):
        for row_pos in range(extent):
            for col_pos in range(extent):
                triple = face_point(face_kind, row_pos, col_pos, extent)
                point_idx = (triple[0] * extent + triple[1]) * extent + triple[2]
                select[point_idx, face_kind * square + row_pos * extent + col_pos] = 1.0
    for code_value in range(8):
        for row_pos in range(extent):
            for col_pos in range(extent):
                row_src = extent - 1 - row_pos if code_value % 2 == 1 else row_pos
                col_src = extent - 1 - col_pos if code_value // 2 % 2 == 1 else col_pos
                if code_value >= 4:
                    source = col_src * extent + row_src
                else:
                    source = row_src * extent + col_src
                rotations[source, code_value * square + row_pos * extent + col_pos] = 1.0
    return (
        jnp.asarray(forward, dtype=jnp.float32),
        jnp.asarray(backward, dtype=jnp.float32),
        jnp.asarray(select, dtype=jnp.float32),
        jnp.asarray(rotations, dtype=jnp.float32),
    )


def stiffness(field_in, geom_cat, mass_term, forward, backward):
    gradients = jnp.dot(field_in, forward, precision=highest, preferred_element_type=jnp.float32)
    return (
        jnp.dot(
            gradients * geom_cat, backward, precision=highest, preferred_element_type=jnp.float32
        )
        + mass_term * field_in
    )


def local_faces(local_out, select):
    face_vals = jnp.dot(local_out, select, precision=highest, preferred_element_type=jnp.float32)
    return face_vals.reshape(face_vals.shape[:-1] + (6, face_vals.shape[-1] // 6))


def shift_lower(values, direction):
    extent = values.shape[direction]
    leading = jnp.zeros_like(lax.slice_in_dim(values, 0, 1, axis=direction))
    return jnp.concatenate(
        [leading, lax.slice_in_dim(values, 0, extent - 1, axis=direction)], axis=direction
    )


def shift_upper(values, direction):
    extent = values.shape[direction]
    trailing = jnp.zeros_like(lax.slice_in_dim(values, 0, 1, axis=direction))
    return jnp.concatenate(
        [lax.slice_in_dim(values, 1, extent, axis=direction), trailing], axis=direction
    )


def assemble(local_out, incoming, orient_block, select, rotations):
    rotated = jnp.dot(incoming, rotations, precision=highest, preferred_element_type=jnp.float32)
    rotated = rotated.reshape(incoming.shape[:-1] + (8, incoming.shape[-1]))
    chosen_mask = orient_block[..., None] == jnp.arange(8, dtype=jnp.int32)
    chosen = jnp.sum(jnp.where(chosen_mask[..., None], rotated, 0.0), axis=-2)
    flattened = chosen.reshape(chosen.shape[:-2] + (chosen.shape[-2] * chosen.shape[-1],))
    return local_out + jnp.dot(
        flattened, select.T, precision=highest, preferred_element_type=jnp.float32
    )


def on_device(old_basis, restart_coeffs, geometry, orientation):
    forward, backward, select, rotations = spectral_tables(NP)
    kept = old_basis.shape[0]
    elements = old_basis.shape[1]
    points = old_basis.shape[2]
    total = float(elements * points * lax.axis_size("wide") * lax.axis_size("narrow"))
    geom_cat = jnp.concatenate([geometry[0], geometry[1], geometry[2]], axis=-1)
    mass_term = geometry[3]
    orient_block = orientation.T.reshape(EX, EY, EZ, 6)
    flat_basis = old_basis.reshape(kept, -1)

    def operate(vector):
        local_out = stiffness(vector, geom_cat, mass_term, forward, backward).reshape(
            EX, EY, EZ, points
        )
        face_vals = local_faces(local_out, select)
        padded = padded_2(face_vals[..., 2:6, :], (("wide", 2), ("narrow", 1)), 1)
        lower_y = padded[:, 0:1, 1 : EZ + 1, 1]
        upper_y = padded[:, EY + 1 : EY + 2, 1 : EZ + 1, 0]
        lower_z = padded[:, 1 : EY + 1, 0:1, 3]
        upper_z = padded[:, 1 : EY + 1, EZ + 1 : EZ + 2, 2]
        incoming = jnp.stack(
            [
                shift_lower(face_vals[..., 1, :], 0),
                shift_upper(face_vals[..., 0, :], 0),
                jnp.concatenate([lower_y, face_vals[:, : EY - 1, :, 3]], axis=1),
                jnp.concatenate([face_vals[:, 1:, :, 2], upper_y], axis=1),
                jnp.concatenate([lower_z, face_vals[:, :, : EZ - 1, 5]], axis=2),
                jnp.concatenate([face_vals[:, :, 1:, 4], upper_z], axis=2),
            ],
            axis=-2,
        )
        return assemble(local_out, incoming, orient_block, select, rotations).reshape(
            elements, points
        )

    def inner(vector):
        return jnp.dot(
            flat_basis, vector.reshape(-1), precision=highest, preferred_element_type=jnp.float32
        )

    def combine(weights):
        return jnp.einsum(
            "k,kep->ep", weights, old_basis, precision=highest, preferred_element_type=jnp.float32
        )

    start_vec = combine(restart_coeffs)
    image_one = operate(start_vec)
    local_terms = (inner(image_one),)
    first_proj = lax.psum(local_terms, ("wide", "narrow"))[0] / total
    residue_one = image_one - combine(first_proj)
    image_raw = operate(residue_one)
    squares, along_basis, along_self = lax.psum(
        (jnp.sum(residue_one * residue_one), inner(image_raw), jnp.sum(residue_one * image_raw)),
        ("wide", "narrow"),
    )
    first_norm = jnp.sqrt(squares / total + epsilon)
    first_vec = residue_one / first_norm
    image_two = image_raw / first_norm
    second_proj = along_basis / total / first_norm
    second_self = along_self / total / (first_norm * first_norm)
    residue_two = image_two - combine(second_proj) - second_self * first_vec
    second_norm = jnp.sqrt(
        lax.psum(jnp.sum(residue_two * residue_two), ("wide", "narrow")) / total + epsilon
    )
    second_vec = residue_two / second_norm
    new_basis = jnp.stack([first_vec, second_vec])
    row_first = jnp.concatenate([first_proj, jnp.stack([first_norm, jnp.zeros_like(first_norm)])])
    row_second = jnp.concatenate([second_proj, jnp.stack([second_self, second_norm])])
    return (new_basis, jnp.stack([row_first, row_second]))


def solution(mesh):
    in_specs = (
        P(None, ("wide", "narrow"), None),
        P(),
        P(None, ("wide", "narrow"), None),
        P(None, ("wide", "narrow")),
    )
    out_specs = (P(None, ("wide", "narrow"), None), P())
    return jax.shard_map(
        on_device, mesh=mesh, in_specs=in_specs, out_specs=out_specs, check_vma=False
    )
```

profile of v0, /device:TPU:0, one launch (start us, length us, event | category | flops | bytes accessed | tf_op | source)
XLA Modules:
  0.0 233.1 jit_solution(17506344067407345133)
XLA Ops:
  0.6 1.1 slice_bitcast_fusion.2
  1.7 3.8 %fusion.4 = f32[1,64,512]{2,0,1:T(1,128)S(1)} fusion(f32[16,64,512]{2,1,0:T(8,128)} %param.8, f32[16]{0:T(128)S(1)} %copy-done), kind=kOutput, calls=%fused_computation.6 | convolution fusion | flops 6291456 | bytes 2228288 | tf_op jit(solution)/shard_map/k,kep->ep/dot_general | solution.py:194
  5.5 4.1 %convolution_multiply_fusion.1 = f32[64,1536]{1,0:T(8,128)S(1)} fusion(f32[512,1536]{1,0:T(8,128)} %constant.23.clone, f32[64,512]{1,0:T(8,128)S(1)} %get-tuple-element.11, f32[64,512]{1,0:T(8,128)S(1)} %get-tuple-element.10, f32[64,512]{1,0:T(8,128)S(1)} %get-tuple-element.9, f32[1,64,512]{2,0,1:T(1,128)S(1)} %fusion.4), kind=kOutput, calls=%fused_computation.1 | convolution fusion | flops 604274688 | bytes 4063232 | tf_op jit(solution)/shard_map/dot_general | solution.py:111
  9.6 3.0 %convolution_add_fusion.3 = f32[64,512]{1,0:T(8,128)S(1)} fusion(f32[64,1536]{1,0:T(8,128)S(1)} %convolution_multiply_fusion.1, f32[1536,512]{1,0:T(8,128)S(1)} %copy-done.2, f32[1,64,512]{2,0,1:T(1,128)S(1)} %fusion.4, f32[4,64,512]{2,1,0:T(8,128)} %param.10), kind=kOutput, calls=%fused_computation.13 | convolution fusion | flops 604045312 | bytes 3932160 | tf_op jit(solution)/shard_map/dot_general | solution.py:113
  13.9 2.3 fusion.13
  16.3 1.3 collective-permute-start.1
  17.6 5.5 %collective-permute-start = (f32[4,4,1,4,64]{4,1,0,3,2:T(4,128)S(1)}, f32[4,4,1,4,64]{4,1,0,3,2:T(4,128)S(1)}, u32[]{:S(2)}, u32[]{:S(2)}) collective-permute-start(f32[4,4,1,4,64]{4,1,0,3,2:T(4,128)S(1)} %copy.108), channel_id=1, source_target_pairs={{0,4},{4,8},{8,12},{12,16},{16,20},{20,24},{24,28},{1,5},{5,9},{9,... | collective-permute-start | bytes 49160 | tf_op jit(solution)/shard_map/ppermute | solution.py:22
  23.5 1.2 collective-permute-done
  24.8 1.3 collective-permute-start.2
  26.1 1.6 reshape.43
  27.7 2.5 %copy.122 = f32[2,8,64,512]{3,1,2,0:T(8,128)} copy(f32[2,8,64,512]{3,2,1,0:T(8,128)S(1)} %bitcast.192) | data formatting | bytes 4194304
  30.3 1.5 collective-permute-start.3
  31.8 3.9 %collective-permute-done.3 = f32[4,1,6,4,64]{4,2,0,3,1:T(8,128)S(1)} collective-permute-done((f32[4,1,6,4,64]{4,2,0,3,1:T(8,128)S(1)}, f32[4,1,6,4,64]{4,2,0,3,1:T(8,128)S(1)}, u32[]{:S(2)}, u32[]{:S(2)}) %collective-permute-start.3) | collective-permute-done | bytes 24608 | tf_op jit(solution)/shard_map/ppermute | solution.py:25
  35.8 1.8 fusion.8
  37.6 2.8 %reshape.44 = f32[4,4,4,6,8,64]{5,4,2,3,1,0:T(8,128)} reshape(f32[4,4,4,6,512]{4,2,3,1,0:T(4,128)} %fusion.8) | data formatting | bytes 1572864 | tf_op jit(solution)/shard_map/reshape | solution.py:143
  40.4 1.9 select_reduce_fusion.1
  42.3 0.7 copy.76
  43.1 1.7 reshape.45
  44.8 1.9 convolution_add_fusion.1
  46.7 0.8 reshape.58
  47.5 4.2 %convolution_bitcast_fusion.1 = f32[16]{0:T(128)S(1)} fusion(f32[32768,1]{0,1:T(1,128)} %reshape.58, f32[16,32768]{1,0:T(8,128)} %bitcast.193), kind=kOutput, calls=%fused_computation.15 | convolution fusion | flops 6291456 | bytes 2228288 | tf_op jit(solution)/shard_map/dot_general | solution.py:189
  51.7 0.7 reshape.46
  52.4 43.2 %psum.35 = f32[16]{0:T(128)S(1)} all-reduce(f32[16]{0:T(128)S(1)} %convolution_bitcast_fusion.1), channel_id=1, replica_groups=mesh['wide'=8,'narrow'=4] {'wide','narrow'}, use_global_device_ids=true, to_apply=%region_1.2 | all-reduce | flops 16 | bytes 128 | tf_op jit(solution)/shard_map/psum | solution.py:201
  95.6 2.2 fusion.2
  97.9 4.1 %convolution_multiply_fusion = f32[64,1536]{1,0:T(8,128)S(1)} fusion(f32[64,512]{1,0:T(8,128)S(1)} %bitcast_subtract_fusion.1, f32[512,1536]{1,0:T(8,128)} %constant.23.clone, f32[64,512]{1,0:T(8,128)S(1)} %get-tuple-element.11, f32[64,512]{1,0:T(8,128)S(1)} %get-tuple-element.10, f32[64,512]{1,0:T(8,128)S(1)} %get-tuple-element.9), kind=kOutput, calls=%fused_computation | convolution fusion | flops 604274688 | bytes 4063232 | tf_op jit(solution)/shard_map/dot_general | solution.py:111
  102.0 2.9 %convolution_add_fusion.2 = f32[64,512]{1,0:T(8,128)S(1)} fusion(f32[64,1536]{1,0:T(8,128)S(1)} %convolution_multiply_fusion, f32[1536,512]{1,0:T(8,128)S(1)} %copy-done.3, f32[64,512]{1,0:T(8,128)S(1)} %bitcast_subtract_fusion.1, f32[4,64,512]{2,1,0:T(8,128)} %param.10), kind=kOutput, calls=%fused_computation.12 | convolution fusion | flops 604045312 | bytes 3932160 | tf_op jit(solution)/shard_map/dot_general | solution.py:113
  105.0 2.5 %fusion.11 = f32[4,4,4,6,64]{4,2,3,1,0:T(4,128)S(1)} fusion(f32[6,64,512,1,1]{2,1,0,4,3:T(8,128)} %constant.37, f32[4,4,4,512,1]{3,2,1,0,4:T(4,128)S(1)} %reshape.62), kind=kOutput, calls=%fused_computation.36 | convolution fusion | flops 150994944 | bytes 1015808 | tf_op jit(solution)/shard_map/dot_general | solution.py:121
  108.3 1.3 collective-permute-start.5
  109.6 4.8 %collective-permute-start.4 = (f32[4,4,1,4,64]{4,1,0,3,2:T(4,128)S(1)}, f32[4,4,1,4,64]{4,1,0,3,2:T(4,128)S(1)}, u32[]{:S(2)}, u32[]{:S(2)}) collective-permute-start(f32[4,4,1,4,64]{4,1,0,3,2:T(4,128)S(1)} %copy.116), channel_id=1, source_target_pairs={{0,4},{4,8},{8,12},{12,16},{16,20},{20,24},{24,28},{1,5},{5,9},{9,... | collective-permute-start | bytes 49160 | tf_op jit(solution)/shard_map/ppermute | solution.py:22
  115.0 1.0 collective-permute-done.4
  116.0 0.7 pad_maximum_fusion.2
  116.7 1.9 collective-permute-start.6
  119.3 0.7 slice.189
  120.0 1.6 collective-permute-start.7
  121.6 0.7 slice.186
  122.3 0.7 slice_bitcast_fusion.16
  123.0 1.4 fusion.20
  124.4 0.7 collective-permute-done.7
  126.9 2.7 %fusion.6 = f32[4,4,4,6,512]{4,2,3,1,0:T(4,128)} fusion(f32[64,512,1,1,1]{1,0,4,3,2:T(8,128)S(1)} %copy-done.8, f32[4,4,4,6,64]{4,2,1,0,3:T(4,128)} %fusion.23), kind=kOutput, calls=%fused_computation.18 | convolution fusion | flops 150994944 | bytes 1015808 | tf_op jit(solution)/shard_map/dot_general | solution.py:142
  129.6 2.7 %reshape.49 = f32[4,4,4,6,8,64]{5,4,2,3,1,0:T(8,128)} reshape(f32[4,4,4,6,512]{4,2,3,1,0:T(4,128)} %fusion.6) | data formatting | bytes 1572864 | tf_op jit(solution)/shard_map/reshape | solution.py:143
  132.4 1.9 select_reduce_fusion
  134.5 0.9 convolution_add_fusion
  135.6 4.1 %convolution_bitcast_fusion = f32[16]{0:T(128)S(1)} fusion(f32[32768,1]{0,1:T(1,128)S(1)} %reshape.63, f32[16,32768]{1,0:T(8,128)} %bitcast.194), kind=kOutput, calls=%fused_computation.14 | convolution fusion | flops 6291456 | bytes 2228288 | tf_op jit(solution)/shard_map/dot_general | solution.py:189
  140.4 44.5 %all-reduce.4 = (f32[16]{0:T(128)S(1)}, f32[]{:T(128)}, f32[]{:T(128)}) all-reduce(f32[16]{0:T(128)S(1)} %convolution_bitcast_fusion, f32[]{:T(128)} %get-tuple-element.3, f32[]{:T(128)} %get-tuple-element.2), channel_id=1, replica_groups=mesh['wide'=8,'narrow'=4] {'wide','narrow'}, use_global_device_ids=true, to_apply=%region_5.6 | all-reduce | flops 18 | bytes 144 | tf_op jit(solution)/shard_map/psum | solution.py:204
  186.3 2.2 fusion
  188.6 0.7 multiply_reduce_fusion
  189.3 41.6 %psum.39 = f32[]{:T(128)} all-reduce(f32[]{:T(128)} %get-tuple-element.7), channel_id=1, replica_groups=mesh['wide'=8,'narrow'=4] {'wide','narrow'}, use_global_device_ids=true, to_apply=%region_9.10 | all-reduce | flops 1 | bytes 8 | tf_op jit(solution)/shard_map/psum | solution.py:215
  232.4 0.7 pad_maximum_fusion.1
  (81 shorter events, 7.8 us)
Async XLA Ops:
  0.6 1.1 copy-start
  5.5 4.1 %copy-start.2 = (f32[1536,512]{1,0:T(8,128)S(1)}, f32[1536,512]{1,0:T(8,128)}, u32[]{:S(2)}) copy-start(f32[1536,512]{1,0:T(8,128)} %constant.24.clone) | copy-start | bytes 9437188
  9.6 4.3 %copy-start.5 = (f32[6,64,512,1,1]{2,1,0,4,3:T(8,128)S(1)}, f32[6,64,512,1,1]{2,1,0,4,3:T(8,128)}, u32[]{:S(2)}) copy-start(f32[6,64,512,1,1]{2,1,0,4,3:T(8,128)} %constant.37) | copy-start | bytes 2359300
  9.6 13.6 %copy-start.12 = (s32[6,64]{1,0:T(8,128)S(1)}, s32[6,64]{1,0:T(8,128)}, u32[]{:S(2)}) copy-start(s32[6,64]{1,0:T(8,128)} %param.11) | copy-start | bytes 4612
  12.6 0.7 copy-start.6
  13.2 14.5 %copy-start.1 = (f32[16,64,512]{2,1,0:T(8,128)S(1)}, f32[16,64,512]{2,1,0:T(8,128)}, u32[]{:S(2)}) copy-start(f32[16,64,512]{2,1,0:T(8,128)} %param.8) | copy-start | bytes 6291460
  16.3 8.4 %collective-permute-start.1 = (f32[4,4,1,4,64]{4,2,0,3,1:T(1,128)S(1)}, f32[4,4,1,4,64]{4,2,0,3,1:T(1,128)S(1)}, u32[]{:S(2)}, u32[]{:S(2)}) collective-permute-start(f32[4,4,1,4,64]{4,2,0,3,1:T(1,128)S(1)} %copy.110), channel_id=1, source_target_pairs={{4,0},{8,4},{12,8},{16,12},{20,16},{24,20},{28,24},{5,1},{9,5},{13... | collective-permute-start | bytes 49160 | tf_op jit(solution)/shard_map/ppermute | solution.py:25
  17.6 7.1 %collective-permute-start = (f32[4,4,1,4,64]{4,1,0,3,2:T(4,128)S(1)}, f32[4,4,1,4,64]{4,1,0,3,2:T(4,128)S(1)}, u32[]{:S(2)}, u32[]{:S(2)}) collective-permute-start(f32[4,4,1,4,64]{4,1,0,3,2:T(4,128)S(1)} %copy.108), channel_id=1, source_target_pairs={{0,4},{4,8},{8,12},{12,16},{16,20},{20,24},{24,28},{1,5},{5,9},{9,... | collective-permute-start | bytes 49160 | tf_op jit(solution)/shard_map/ppermute | solution.py:22
  24.8 7.0 %collective-permute-start.2 = (f32[4,1,6,4,64]{4,2,0,3,1:T(8,128)S(1)}, f32[4,1,6,4,64]{4,2,0,3,1:T(8,128)S(1)}, u32[]{:S(2)}, u32[]{:S(2)}) collective-permute-start(f32[4,1,6,4,64]{4,2,0,3,1:T(8,128)S(1)} %get-tuple-element.27), channel_id=1, source_target_pairs={{0,1},{1,2},{2,3},{4,5},{5,6},{6,7},{8,9},{9,10},{10,11},{12,13},{... | collective-permute-start | bytes 73736 | tf_op jit(solution)/shard_map/ppermute | solution.py:22
  27.7 8.1 %copy-start.7 = (f32[64,512,1,1,1]{1,0,4,3,2:T(8,128)S(1)}, f32[64,512,1,1,1]{1,0,4,3,2:T(8,128)}, u32[]{:S(2)}) copy-start(f32[64,512,1,1,1]{1,0,4,3,2:T(8,128)} %constant.38) | copy-start | bytes 393220
  30.3 5.4 %collective-permute-start.3 = (f32[4,1,6,4,64]{4,2,0,3,1:T(8,128)S(1)}, f32[4,1,6,4,64]{4,2,0,3,1:T(8,128)S(1)}, u32[]{:S(2)}, u32[]{:S(2)}) collective-permute-start(f32[4,1,6,4,64]{4,2,0,3,1:T(8,128)S(1)} %get-tuple-element.26), channel_id=1, source_target_pairs={{1,0},{2,1},{3,2},{5,4},{6,5},{7,6},{9,8},{10,9},{11,10},{13,12},{... | collective-permute-start | bytes 73736 | tf_op jit(solution)/shard_map/ppermute | solution.py:25
  37.6 7.2 %copy-start.4 = (f32[512,384,1,1]{1,0,3,2:T(8,128)S(1)}, f32[512,384,1,1]{1,0,3,2:T(8,128)}, u32[]{:S(2)}) copy-start(f32[512,384,1,1]{1,0,3,2:T(8,128)} %constant.39) | copy-start | bytes 2359300
  95.6 2.3 copy-start.9
  97.9 4.1 %copy-start.3 = (f32[1536,512]{1,0:T(8,128)S(1)}, f32[1536,512]{1,0:T(8,128)}, u32[]{:S(2)}) copy-start(f32[1536,512]{1,0:T(8,128)} %constant.24.clone) | copy-start | bytes 9437188
  104.9 22.0 %copy-start.8 = (f32[64,512,1,1,1]{1,0,4,3,2:T(8,128)S(1)}, f32[64,512,1,1,1]{1,0,4,3,2:T(8,128)}, u32[]{:S(2)}) copy-start(f32[64,512,1,1,1]{1,0,4,3,2:T(8,128)} %constant.38) | copy-start | bytes 393220
  108.3 7.7 %collective-permute-start.5 = (f32[4,4,1,4,64]{4,2,0,3,1:T(1,128)S(1)}, f32[4,4,1,4,64]{4,2,0,3,1:T(1,128)S(1)}, u32[]{:S(2)}, u32[]{:S(2)}) collective-permute-start(f32[4,4,1,4,64]{4,2,0,3,1:T(1,128)S(1)} %copy.118), channel_id=1, source_target_pairs={{4,0},{8,4},{12,8},{16,12},{20,16},{24,20},{28,24},{5,1},{9,5},{13... | collective-permute-start | bytes 49160 | tf_op jit(solution)/shard_map/ppermute | solution.py:25
  109.6 6.4 %collective-permute-start.4 = (f32[4,4,1,4,64]{4,1,0,3,2:T(4,128)S(1)}, f32[4,4,1,4,64]{4,1,0,3,2:T(4,128)S(1)}, u32[]{:S(2)}, u32[]{:S(2)}) collective-permute-start(f32[4,4,1,4,64]{4,1,0,3,2:T(4,128)S(1)} %copy.116), channel_id=1, source_target_pairs={{0,4},{4,8},{8,12},{12,16},{16,20},{20,24},{24,28},{1,5},{5,9},{9,... | collective-permute-start | bytes 49160 | tf_op jit(solution)/shard_map/ppermute | solution.py:22
  116.0 2.7 %copy-start.11 = (f32[4,4,1,4,64]{4,1,0,3,2:T(4,128)}, f32[4,4,1,4,64]{4,1,0,3,2:T(4,128)S(1)}, u32[]{:S(2)}) copy-start(f32[4,4,1,4,64]{4,1,0,3,2:T(4,128)S(1)} %collective-permute-done.4) | copy-start | bytes 49156
  116.0 2.6 %copy-start.10 = (f32[4,4,1,4,64]{4,2,0,3,1:T(1,128)}, f32[4,4,1,4,64]{4,2,0,3,1:T(1,128)S(1)}, u32[]{:S(2)}) copy-start(f32[4,4,1,4,64]{4,2,0,3,1:T(1,128)S(1)} %collective-permute-done.5) | copy-start | bytes 49156
  116.7 5.5 %collective-permute-start.6 = (f32[4,1,6,4,64]{4,2,0,3,1:T(8,128)}, f32[4,1,6,4,64]{4,2,0,3,1:T(8,128)}, u32[]{:S(2)}, u32[]{:S(2)}) collective-permute-start(f32[4,1,6,4,64]{4,2,0,3,1:T(8,128)} %get-tuple-element.17), channel_id=1, source_target_pairs={{0,1},{1,2},{2,3},{4,5},{5,6},{6,7},{8,9},{9,10},{10,11},{12,13},{... | collective-permute-start | bytes 73736 | tf_op jit(solution)/shard_map/ppermute | solution.py:22
  120.0 5.0 %collective-permute-start.7 = (f32[4,1,6,4,64]{4,2,0,3,1:T(8,128)}, f32[4,1,6,4,64]{4,2,0,3,1:T(8,128)S(1)}, u32[]{:S(2)}, u32[]{:S(2)}) collective-permute-start(f32[4,1,6,4,64]{4,2,0,3,1:T(8,128)} %get-tuple-element.16), channel_id=1, source_target_pairs={{1,0},{2,1},{3,2},{5,4},{6,5},{7,6},{9,8},{10,9},{11,10},{13,12},{... | collective-permute-start | bytes 73736 | tf_op jit(solution)/shard_map/ppermute | solution.py:25
where the time goes:
time: 234 us; the launch traced here: 233 us
  blocking collectives  129 us (55%)
  matrix products  42.7 us (18%)
  local copies, waits for them, and re-layouts  21 us (9%)
  starting transfers between devices  19.1 us (8%)
  other arithmetic  11 us (5%)
  waiting for transfers between devices  6.7 us (3%)
  between operations  3.2 us (1%)
    psum x1, blocking collectives, on_device(): lax.psum((jnp.sum(residue_one * residue_one), inner(image_raw), jnp.sum(r...  44.5 us
    psum x1, blocking collectives, on_device(): first_proj = lax.psum(local_terms, ('wide', 'narrow'))[0] / total  43.2 us
    psum x1, blocking collectives, on_device(): lax.psum(jnp.sum(residue_two * residue_two), ('wide', 'narrow')) / total  41.6 us
    ppermute x4, starting transfers between devices, padded_2(): lax.ppermute(lax.slice_in_dim(block, block.shape[dim] - width, None, axis...  13.5 us
    dot_general x2, matrix products, inner(): jnp.dot(flat_basis, vector.reshape(-1), precision=highest, preferred_elem...  8.35 us
    dot_general x3, matrix products, combine(): jnp.einsum('k,kep->ep', weights, old_basis, precision=highest, preferred_...  8.24 us
    dot_general x2, matrix products, stiffness(): jnp.dot(field_in, forward, precision=highest, preferred_element_type=jnp....  8.11 us
    dot_general x2, matrix products, stiffness(): jnp.dot(gradients * geom_cat, backward, precision=highest, preferred_elem...  5.89 us
  transfers between devices with their start and end apart: 8, of which 4 were waited for; matrix products, arithmetic and copies ran while one was open for 4% of the time, Pallas kernels for 0%

commit v1 on v0

v1 whole, which is shorter than its diff:
```python
import functools

import jax
import jax.numpy as jnp
import numpy as np
from jax import lax
from jax.experimental import pallas as pl
from jax.experimental.pallas import tpu as pltpu
from jax.sharding import PartitionSpec as P

NP = 8
EX = 4
EY = 4
EZ = 4
LANES = 128
FACE = NP * NP
MESH = pl.DeviceIdType.MESH
highest = lax.Precision.HIGHEST
epsilon = 1e-06


def legendre_columns(nodes, degree):
    columns = [nodes * 0.0 + 1.0, nodes * 1.0]
    for order in range(2, degree + 1):
        columns.append(
            ((2 * order - 1) * nodes * columns[order - 1] - (order - 1) * columns[order - 2])
            / order
        )
    return columns


def gll_derivative(extent):
    degree = extent - 1
    nodes = np.cos(np.pi * np.arange(extent) / degree)
    for sweep in range(100):
        columns = legendre_columns(nodes, degree)
        nodes = nodes - (nodes * columns[degree] - columns[degree - 1]) / (extent * columns[degree])
    gll_nodes = nodes[::-1] * 1.0
    values = legendre_columns(gll_nodes, degree)[degree]
    matrix = np.zeros((extent, extent))
    for row_idx in range(extent):
        for col_idx in range(extent):
            if row_idx != col_idx:
                matrix[row_idx, col_idx] = values[row_idx] / (
                    values[col_idx] * (gll_nodes[row_idx] - gll_nodes[col_idx])
                )
    matrix[0, 0] = -degree * (degree + 1) / 4.0
    matrix[extent - 1, extent - 1] = degree * (degree + 1) / 4.0
    return matrix


def tables():
    matrix = gll_derivative(NP)
    identity = np.eye(NP)
    pair = np.eye(2)
    along_y = np.kron(pair, np.kron(matrix, identity))
    along_z = np.kron(pair, np.kron(identity, matrix))
    forward = np.concatenate([along_y.T, along_z.T], axis=1)
    backward = np.concatenate([along_y, along_z], axis=0)
    tiles = NP // 2
    coef = np.zeros((2, tiles, tiles, 2, LANES))
    for way, table in enumerate((matrix, matrix.T)):
        for out_tile in range(tiles):
            for in_tile in range(tiles):
                for half in range(2):
                    lanes = slice(half * FACE, (half + 1) * FACE)
                    row = 2 * out_tile + half
                    coef[way, out_tile, in_tile, 0, lanes] = table[row, 2 * in_tile + half]
                    coef[way, out_tile, in_tile, 1, lanes] = table[row, 2 * in_tile + 1 - half]
    return (
        jnp.asarray(forward, jnp.float32),
        jnp.asarray(backward, jnp.float32),
        jnp.asarray(coef.reshape(-1, LANES), jnp.float32),
    )


def take_lanes(values, index):
    return jnp.take_along_axis(values, index, axis=1, mode="promise_in_bounds")


def rotated(row, col, code):
    row = row ^ (7 * (code & 1))
    col = col ^ (7 * ((code >> 1) & 1))
    return jnp.where((code & 4) != 0, col * NP + row, row * NP + col)


def kernel(
    n_wide,
    n_narrow,
    coeffs,
    basis_hbm,
    geom_hbm,
    orient,
    forward_hbm,
    backward_hbm,
    coef_hbm,
    out,
    hess,
    basis,
    geom,
    forward,
    backward,
    coef,
    index,
    orient_pad,
    image,
    first,
    face_y,
    face_z,
    halo_y,
    halo_z,
    outbox,
    inbox,
    row_out,
    row_in,
    load_sem,
    halo_send,
    halo_recv,
    row_send,
    row_recv,
):
    wide = lax.axis_index("wide")
    narrow = lax.axis_index("narrow")
    devices = n_wide * n_narrow
    me = wide * n_narrow + narrow
    kept, elements, points = basis.shape
    tiles = points // LANES
    total = float(elements * points * devices)

    def load(source, target, slot):
        return pltpu.make_async_copy(source, target, load_sem.at[slot])

    chunk = kept // 4
    loads = [
        load(basis_hbm.at[pl.ds(part * chunk, chunk)], basis.at[pl.ds(part * chunk, chunk)], part)
        for part in range(4)
    ]
    loads += [
        load(forward_hbm, forward, 4),
        load(geom_hbm, geom, 5),
        load(backward_hbm, backward, 6),
        load(coef_hbm, coef, 7),
    ]
    for copy in loads:
        copy.start()

    inbox[...] = jnp.zeros_like(inbox)

    def peer(step):
        other = lax.rem(me + step, devices)
        return (other // n_narrow, lax.rem(other, n_narrow))

    barrier = pltpu.get_barrier_semaphore()

    def greet(step, carry):
        pl.semaphore_signal(barrier, inc=1, device_id=peer(step), device_id_type=MESH)
        return carry

    lax.fori_loop(1, devices, greet, 0)

    lane = lax.broadcasted_iota(jnp.int32, (elements, LANES), 1)
    line = lax.broadcasted_iota(jnp.int32, (elements, LANES), 0)
    low_half = lane < FACE
    half = lane // FACE
    mid = (lane // NP) % NP
    fast = lane % NP
    row_y = (line // EZ) % EY
    row_z = line % EZ
    at_y = (mid == 0) | (mid == NP - 1)
    at_z = (fast == 0) | (fast == NP - 1)

    orient_pad[...] = jnp.zeros_like(orient_pad)
    orient_pad[pl.ds(0, 6), pl.ds(0, elements)] = orient[...]
    codes = jnp.transpose(orient_pad[...])[:elements]
    code = [jnp.broadcast_to(codes[:, f : f + 1], (elements, LANES)) for f in range(6)]
    code_x = jnp.where(low_half, code[0], code[1])
    index[2 * tiles] = rotated(mid, fast, code_x) + jnp.where(low_half, FACE, 0)
    code_y = jnp.where(mid == 0, code[2], code[3])
    code_z = jnp.where(fast == 0, code[4], code[5])
    for tile in range(tiles):
        first_pos = 2 * tile + half
        index[tile] = rotated(first_pos, fast, code_y) + jnp.where(mid == 0, FACE, 0)
        index[tiles + tile] = rotated(first_pos, mid, code_z) + jnp.where(fast == 0, FACE, 0)

    pick_y = (mid % 2) * FACE + half * (FACE - NP) + fast
    pick_z = (mid % 2) * FACE + fast * NP + half * (NP - 1)
    source_tile = mid // 2

    def tile_of(values, tile):
        return values[:, tile * LANES : (tile + 1) * LANES]

    def swap(values):
        return pltpu.roll(values, FACE, axis=1)

    def along_x(parts, way):
        swapped = [swap(part) for part in parts]
        outs = []
        for out_tile in range(tiles):
            acc = None
            for in_tile in range(tiles):
                at = ((way * tiles + out_tile) * tiles + in_tile) * 2
                term = (
                    coef[pl.ds(at, 1), :] * parts[in_tile]
                    + coef[pl.ds(at + 1, 1), :] * swapped[in_tile]
                )
                acc = term if acc is None else acc + term
            outs.append(acc)
        return outs

    def local(parts):
        stacked = jnp.concatenate(parts, axis=0)
        grads = jnp.dot(
            stacked, forward[...], precision=highest, preferred_element_type=jnp.float32
        )
        geom_y = jnp.concatenate([geom[1, :, pl.ds(t * LANES, LANES)] for t in range(tiles)], axis=0)
        geom_z = jnp.concatenate([geom[2, :, pl.ds(t * LANES, LANES)] for t in range(tiles)], axis=0)
        flux = jnp.concatenate([grads[:, :LANES] * geom_y, grads[:, LANES:] * geom_z], axis=1)
        back = jnp.dot(
            flux, backward[...], precision=highest, preferred_element_type=jnp.float32
        )
        grad_x = along_x(parts, 0)
        flux_x = [grad_x[t] * geom[0, :, pl.ds(t * LANES, LANES)] for t in range(tiles)]
        back_x = along_x(flux_x, 1)
        return [
            back[t * elements : (t + 1) * elements]
            + back_x[t]
            + geom[3, :, pl.ds(t * LANES, LANES)] * parts[t]
            for t in range(tiles)
        ]

    def faces(parts, pick):
        found = take_lanes(parts[0], pick)
        for tile in range(1, tiles):
            found = jnp.where(source_tile == tile, take_lanes(parts[tile], pick), found)
        return found

    has = (narrow > 0, narrow < n_narrow - 1, wide > 0, wide < n_wide - 1)
    where_to = ((wide, narrow - 1), (wide, narrow + 1), (wide - 1, narrow), (wide + 1, narrow))

    def face_copy(step, side):
        return pltpu.make_async_remote_copy(
            src_ref=outbox.at[step, side],
            dst_ref=inbox.at[step, side ^ 1],
            send_sem=halo_send.at[step, side],
            recv_sem=halo_recv.at[step, side ^ 1],
            device_id=where_to[side],
            device_id_type=MESH,
        )

    def face_arrival(step, side):
        return pltpu.make_async_copy(
            inbox.at[step, side], inbox.at[step, side], halo_recv.at[step, side]
        )

    def operate(parts, step, ready):
        result = local(parts)
        found_y = faces(result, pick_y)
        found_z = faces(result, pick_z)
        face_y[...] = found_y
        face_z[...] = found_z
        for ex in range(EX):
            outbox[step, 0, pl.ds(ex * EZ, EZ), :] = face_y[pl.ds(ex * EY * EZ, EZ), :]
            outbox[step, 1, pl.ds(ex * EZ, EZ), :] = face_y[pl.ds(ex * EY * EZ + (EY - 1) * EZ, EZ), :]
        outbox[step, 2] = face_z[pl.ds(0, EX * EY, stride=EZ), :]
        outbox[step, 3] = face_z[pl.ds(EZ - 1, EX * EY, stride=EZ), :]
        ready()
        for side in (2, 3, 0, 1):

            @pl.when(has[side])
            def _():
                face_copy(step, side).start()

        face_x = jnp.where(low_half, result[0], result[tiles - 1])
        width = EY * EZ
        blank = jnp.zeros((width, LANES), jnp.float32)
        in_x = jnp.where(
            low_half,
            jnp.concatenate([face_x[width:], blank], axis=0),
            jnp.concatenate([blank, face_x[: elements - width]], axis=0),
        )
        in_y = jnp.where(
            low_half, pltpu.roll(found_y, elements - EZ, axis=0), pltpu.roll(found_y, EZ, axis=0)
        )
        in_z = jnp.where(
            low_half, pltpu.roll(found_z, elements - 1, axis=0), pltpu.roll(found_z, 1, axis=0)
        )
        got_x = take_lanes(in_x, index[2 * tiles])
        result[0] = result[0] + jnp.where(low_half, got_x, 0.0)
        result[tiles - 1] = result[tiles - 1] + jnp.where(low_half, 0.0, got_x)

        for side in range(4):

            @pl.when(has[side])
            def _():
                face_arrival(step, side).wait()

        for ex in range(EX):
            halo_y[pl.ds(ex * EY * EZ, EZ), :] = inbox[step, 0, pl.ds(ex * EZ, EZ), :]
            halo_y[pl.ds(ex * EY * EZ + (EY - 1) * EZ, EZ), :] = inbox[step, 1, pl.ds(ex * EZ, EZ), :]
        halo_z[pl.ds(0, EX * EY, stride=EZ), :] = inbox[step, 2]
        halo_z[pl.ds(EZ - 1, EX * EY, stride=EZ), :] = inbox[step, 3]
        edge_y = row_y == jnp.where(low_half, EY - 1, 0)
        edge_z = row_z == jnp.where(low_half, EZ - 1, 0)
        in_y = jnp.where(edge_y, halo_y[...], in_y)
        in_z = jnp.where(edge_z, halo_z[...], in_z)
        return [
            result[t]
            + jnp.where(at_y, take_lanes(in_y, index[t]), 0.0)
            + jnp.where(at_z, take_lanes(in_z, index[tiles + t]), 0.0)
            for t in range(tiles)
        ]

    def folded(values):
        acc = tile_of(values, 0)
        for tile in range(1, tiles):
            acc = acc + tile_of(values, tile)
        return jnp.sum(acc.reshape(elements // 8, 8, LANES), axis=0)

    def to_row(partials):
        count = -(-len(partials) // 8) * 8
        rows = [jnp.sum(part, axis=0, keepdims=True) for part in partials]
        rows += [jnp.zeros((1, LANES), jnp.float32)] * (count - len(rows))
        block = jnp.concatenate(rows, axis=0)
        sums = jnp.sum(block, axis=1, keepdims=True)
        place = lax.broadcasted_iota(jnp.int32, (count, LANES), 0) == lax.broadcasted_iota(
            jnp.int32, (count, LANES), 1
        )
        return jnp.sum(jnp.where(place, sums, 0.0), axis=0, keepdims=True)

    def all_sum(row, phase):
        row_out[phase] = row
        row_in[phase, pl.ds(me, 1)] = row.reshape(1, 1, LANES)

        def send(step, carry):
            pltpu.make_async_remote_copy(
                src_ref=row_out.at[phase],
                dst_ref=row_in.at[phase, me],
                send_sem=row_send.at[phase],
                recv_sem=row_recv.at[phase],
                device_id=peer(step),
                device_id_type=MESH,
            ).start()
            return carry

        lax.fori_loop(1, devices, send, 0)
        span = row_in.at[phase, pl.ds(0, devices - 1)]
        pltpu.make_async_copy(span, span, row_recv.at[phase]).wait()
        return jnp.sum(row_in[phase], axis=0)

    def weight(row, at):
        return row[:, at : at + 1]

    start = None
    for part in range(4):
        loads[part].wait()
        for at in range(part * chunk, (part + 1) * chunk):
            term = coeffs[at] * basis[at]
            start = term if start is None else start + term
    for copy in loads[4:]:
        copy.wait()

    def greeted():
        pl.semaphore_wait(barrier, devices - 1)

    image_parts = operate([tile_of(start, t) for t in range(tiles)], 0, greeted)
    for t in range(tiles):
        image[:, pl.ds(t * LANES, LANES)] = image_parts[t]
    row = to_row([folded(basis[at] * image[...]) for at in range(kept)])
    proj_one = all_sum(row, 0) / total
    acc = image[...]
    for at in range(kept):
        acc = acc - weight(proj_one, at) * basis[at]
    first[...] = acc

    image_parts = operate(
        [first[:, pl.ds(t * LANES, LANES)] for t in range(tiles)], 1, lambda: None
    )
    for t in range(tiles):
        image[:, pl.ds(t * LANES, LANES)] = image_parts[t]
    row = to_row(
        [folded(basis[at] * image[...]) for at in range(kept)]
        + [folded(first[...] * first[...]), folded(first[...] * image[...])]
    )
    sums = all_sum(row, 1) / total
    norm_one = jnp.sqrt(weight(sums, kept) + epsilon)
    scale_one = 1.0 / norm_one
    proj_two = sums * scale_one
    self_two = weight(sums, kept + 1) * scale_one * scale_one
    acc = image[...] - (self_two * first[...])
    for at in range(kept):
        acc = acc - weight(sums, at) * basis[at]
    acc = acc * scale_one
    out[0] = first[...] * scale_one
    image[...] = acc
    square = all_sum(to_row([folded(acc * acc)]), 2) / total
    norm_two = jnp.sqrt(weight(square, 0) + epsilon)
    out[1] = image[...] * (1.0 / norm_two)

    spot = lax.broadcasted_iota(jnp.int32, (1, LANES), 1)
    row_first = jnp.where(spot < kept, proj_one, jnp.where(spot == kept, norm_one, 0.0))
    row_second = jnp.where(spot < kept, proj_two, jnp.where(spot == kept, self_two, norm_two))
    hess[pl.ds(0, 1), :] = row_first[:, : kept + 2]
    hess[pl.ds(1, 1), :] = row_second[:, : kept + 2]

    for step in range(2):
        for side in range(4):

            @pl.when(has[side])
            def _():
                face_copy(step, side).wait_send()

    for phase in range(3):
        span = row_in.at[phase, pl.ds(0, devices - 1)]
        pltpu.make_async_copy(span, span, row_send.at[phase]).wait()


def on_device(n_wide, n_narrow, old_basis, restart_coeffs, geometry, orientation):
    kept, elements, points = old_basis.shape
    tiles = points // LANES
    devices = n_wide * n_narrow
    forward, backward, coef = tables()
    anywhere = pl.BlockSpec(memory_space=pl.ANY)
    vmem = pl.BlockSpec(memory_space=pltpu.VMEM)
    f32 = jnp.float32
    border = EX * EY
    return pl.pallas_call(
        functools.partial(kernel, n_wide, n_narrow),
        out_shape=(
            jax.ShapeDtypeStruct((2, elements, points), f32),
            jax.ShapeDtypeStruct((2, kept + 2), f32),
        ),
        in_specs=[
            pl.BlockSpec(memory_space=pltpu.SMEM),
            anywhere,
            anywhere,
            vmem,
            anywhere,
            anywhere,
            anywhere,
        ],
        out_specs=(vmem, vmem),
        scratch_shapes=[
            pltpu.VMEM(old_basis.shape, f32),
            pltpu.VMEM(geometry.shape, f32),
            pltpu.VMEM(forward.shape, f32),
            pltpu.VMEM(backward.shape, f32),
            pltpu.VMEM(coef.shape, f32),
            pltpu.VMEM((2 * tiles + 1, elements, LANES), jnp.int32),
            pltpu.VMEM((8, LANES), jnp.int32),
            pltpu.VMEM((elements, points), f32),
            pltpu.VMEM((elements, points), f32),
            pltpu.VMEM((elements, LANES), f32),
            pltpu.VMEM((elements, LANES), f32),
            pltpu.VMEM((elements, LANES), f32),
            pltpu.VMEM((elements, LANES), f32),
            pltpu.VMEM((2, 4, border, LANES), f32),
            pltpu.VMEM((2, 4, border, LANES), f32),
            pltpu.VMEM((3, 1, LANES), f32),
            pltpu.VMEM((3, devices, 1, LANES), f32),
            pltpu.SemaphoreType.DMA((8,)),
            pltpu.SemaphoreType.DMA((2, 4)),
            pltpu.SemaphoreType.DMA((2, 4)),
            pltpu.SemaphoreType.DMA((3,)),
            pltpu.SemaphoreType.DMA((3,)),
        ],
        compiler_params=pltpu.CompilerParams(collective_id=0, has_side_effects=True),
        name="arnoldi",
    )(restart_coeffs, old_basis, geometry, orientation, forward, backward, coef)


def solution(mesh):
    in_specs = (
        P(None, ("wide", "narrow"), None),
        P(),
        P(None, ("wide", "narrow"), None),
        P(None, ("wide", "narrow")),
    )
    out_specs = (P(None, ("wide", "narrow"), None), P())
    return jax.shard_map(
        functools.partial(on_device, mesh.shape["wide"], mesh.shape["narrow"]),
        mesh=mesh,
        in_specs=in_specs,
        out_specs=out_specs,
        check_vma=False,
    )
```

time: 234 us -> 34.5 us (0.15)
  blocking collectives: 129 us -> 0 us
  matrix products: 42.7 us -> 0 us
  Pallas kernels: 0 us -> 30.7 us
  starting transfers between devices: 19.1 us -> 0 us
  local copies, waits for them, and re-layouts: 21 us -> 2.9 us
  other arithmetic: 11 us -> 0 us
  waiting for transfers between devices: 6.7 us -> 0 us
  between operations: 3.2 us -> 0.64 us
    psum x3 -> x0, blocking collectives: 129 us -> none  [the longest x1 44.5 us: on_device(): lax.psum((jnp.sum(residue_one * residue_one), inner(image_raw), jnp.sum(r...]
    dot_general x15 -> x0, matrix products: 42.7 us -> none  [the longest x2 8.35 us: inner(): jnp.dot(flat_basis, vector.reshape(-1), precision=highest, preferred_elem...]
    pallas_call x0 -> x1, Pallas kernels: none -> 30.7 us  [on_device(): pl.pallas_call(functools.partial(kernel, n_wide, n_narrow), out_shape=(ja...]
    ppermute x8 -> x0, starting transfers between devices: 19.1 us -> none  [the longest x4 13.5 us: padded_2(): lax.ppermute(lax.slice_in_dim(block, block.shape[dim] - width, None, axis...]
    reshape x10 -> x0, local copies, waits for them, and re-layouts: 10.4 us -> none  [the longest x2 5.51 us: assemble(): rotated = rotated.reshape(incoming.shape[:-1] + (8, incoming.shape[-1]))]
    ppermute x8 -> x0, waiting for transfers between devices: 6.7 us -> none  [the longest x4 4.57 us: padded_2(): lax.ppermute(lax.slice_in_dim(block, 0, width, axis=dim), axis, backward)]
    reduce_sum x4 -> x0, other arithmetic: 5.23 us -> none  [the longest x2 3.86 us: assemble(): chosen = jnp.sum(jnp.where(chosen_mask[..., None], rotated, 0.0), axis=-2)]
    unnamed x6 -> x0, other arithmetic: 2.69 us -> none
  transfers between devices with their start and end apart: 8 -> 0, of which waited for: 4 -> 0; matrix products, arithmetic and copies ran while one was open for 4% -> 0% of each run, Pallas kernels for 0% -> 0%
where the time goes in v1:
time: 34.5 us; the launch traced here: 34.3 us
  Pallas kernels  30.7 us (89%)
  local copies, waits for them, and re-layouts  2.9 us (8%)
  between operations  0.64 us (2%)
    pallas_call x1, Pallas kernels, on_device(): pl.pallas_call(functools.partial(kernel, n_wide, n_narrow), out_shape=(ja...  30.7 us
    unnamed x2, local copies, waits for them, and re-layouts  2.9 us

profile of v1, /device:TPU:0, one launch (start us, length us, event | category | flops | bytes accessed | tf_op | source)
XLA Modules:
  0.0 34.3 jit_solution(17757066384723759288)
XLA Ops:
  0.6 30.7 %arnoldi.1 = (f32[2,64,512]{2,1,0:T(8,128)}, f32[2,18]{1,0:T(2,128)}) custom-call(f32[16]{0:T(128)} %coeffs.1, f32[16,64,512]{2,1,0:T(8,128)} %basis_hbm.1, f32[4,64,512]{2,1,0:T(8,128)} %geom_hbm.1, s32[6,64]{1,0:T(8,128)} %orient.1, f32[128,256]{1,0:T(8,128)} %constant.6.clone.forward_hbm, f32[256,128]{1,0:T(8,128)} %constant.7.clone.backward_hbm, ...), custom_call_target="tpu_custom_call" | custom-call | tf_op jit(solution)/shard_map/arnoldi/pallas_call | solution.py:426
  31.3 1.7 %copy.11 = f32[2,64,512]{2,1,0:T(8,128)} copy(f32[2,64,512]{2,1,0:T(8,128)} %get-tuple-element.4) | data formatting | bytes 524288
  33.0 1.2 %copy.12 = f32[2,18]{1,0:T(2,128)} copy(f32[2,18]{1,0:T(2,128)} %get-tuple-element.5) | data formatting | bytes 288

commit v2 on v1

--- a/solution.py
+++ b/solution.py
@@ -74,6 +74,19 @@
     )
 
 
+def pair_rows(kept):
+    count = kept + 2
+    listed = [(at, kept + 1) for at in range(count)]
+    listed += [(at, kept) for at in range(kept + 1)]
+    block = 4
+    for left in range(0, kept, block):
+        for right in range(left, kept, block):
+            for one in range(left, left + block):
+                for two in range(max(right, one), right + block):
+                    listed.append((one, two))
+    return -(-len(listed) // LANES), listed
+
+
 def take_lanes(values, index):
     return jnp.take_along_axis(values, index, axis=1, mode="promise_in_bounds")
 
@@ -94,6 +107,7 @@
     forward_hbm,
     backward_hbm,
     coef_hbm,
+    pairs_hbm,
     out,
     hess,
     basis,
@@ -111,8 +125,11 @@
     halo_z,
     outbox,
     inbox,
+    pairs,
     row_out,
     row_in,
+    pair_out,
+    pair_in,
     load_sem,
     halo_send,
     halo_recv,
@@ -140,23 +157,43 @@
         load(geom_hbm, geom, 5),
         load(backward_hbm, backward, 6),
         load(coef_hbm, coef, 7),
+        load(pairs_hbm, pairs, 8),
     ]
     for copy in loads:
         copy.start()
 
+    messages = ((row_out, row_in), (pair_out, pair_in))
     inbox[...] = jnp.zeros_like(inbox)
 
     def peer(step):
-        other = lax.rem(me + step, devices)
+        if devices & (devices - 1):
+            other = lax.rem(me + step, devices)
+        else:
+            other = me
+            for bit in range(devices.bit_length() - 1):
+                if step >> bit & 1:
+                    other = other + (1 - 2 * lax.rem(me // 2**bit, 2)) * 2**bit
         return (other // n_narrow, lax.rem(other, n_narrow))
 
+    def each_peer(act):
+        if devices <= 64:
+            for step in range(devices - 1, 0, -1):
+                act(peer(step))
+        else:
+
+            def body(step, carry):
+                other = lax.rem(me + step, devices)
+                act((other // n_narrow, lax.rem(other, n_narrow)))
+                return carry
+
+            lax.fori_loop(1, devices, body, 0)
+
     barrier = pltpu.get_barrier_semaphore()
 
-    def greet(step, carry):
-        pl.semaphore_signal(barrier, inc=1, device_id=peer(step), device_id_type=MESH)
-        return carry
-
-    lax.fori_loop(1, devices, greet, 0)
+    def greet(where):
+        pl.semaphore_signal(barrier, inc=1, device_id=where, device_id_type=MESH)
+
+    each_peer(greet)
 
     lane = lax.broadcasted_iota(jnp.int32, (elements, LANES), 1)
     line = lax.broadcasted_iota(jnp.int32, (elements, LANES), 0)
@@ -252,7 +289,7 @@
             inbox.at[step, side], inbox.at[step, side], halo_recv.at[step, side]
         )
 
-    def operate(parts, step, ready):
+    def operate(parts, step, ready, beside=lambda: None):
         result = local(parts)
         found_y = faces(result, pick_y)
         found_z = faces(result, pick_z)
@@ -287,6 +324,8 @@
         got_x = take_lanes(in_x, index[2 * tiles])
         result[0] = result[0] + jnp.where(low_half, got_x, 0.0)
         result[tiles - 1] = result[tiles - 1] + jnp.where(low_half, 0.0, got_x)
+
+        beside()
 
         for side in range(4):
 
@@ -316,36 +355,37 @@
             acc = acc + tile_of(values, tile)
         return jnp.sum(acc.reshape(elements // 8, 8, LANES), axis=0)
 
-    def to_row(partials):
+    def to_row(partials, begin=0):
         count = -(-len(partials) // 8) * 8
         rows = [jnp.sum(part, axis=0, keepdims=True) for part in partials]
         rows += [jnp.zeros((1, LANES), jnp.float32)] * (count - len(rows))
         block = jnp.concatenate(rows, axis=0)
         sums = jnp.sum(block, axis=1, keepdims=True)
-        place = lax.broadcasted_iota(jnp.int32, (count, LANES), 0) == lax.broadcasted_iota(
+        place = lax.broadcasted_iota(jnp.int32, (count, LANES), 0) + begin == lax.broadcasted_iota(
             jnp.int32, (count, LANES), 1
         )
         return jnp.sum(jnp.where(place, sums, 0.0), axis=0, keepdims=True)
 
-    def all_sum(row, phase):
-        row_out[phase] = row
-        row_in[phase, pl.ds(me, 1)] = row.reshape(1, 1, LANES)
-
-        def send(step, carry):
+    def all_sum(block, phase, beside):
+        outgoing, incoming = messages[phase]
+        outgoing[...] = block
+        incoming[pl.ds(me, 1)] = block.reshape((1,) + block.shape)
+
+        def send(where):
             pltpu.make_async_remote_copy(
-                src_ref=row_out.at[phase],
-                dst_ref=row_in.at[phase, me],
+                src_ref=outgoing,
+                dst_ref=incoming.at[me],
                 send_sem=row_send.at[phase],
                 recv_sem=row_recv.at[phase],
-                device_id=peer(step),
+                device_id=where,
                 device_id_type=MESH,
             ).start()
-            return carry
-
-        lax.fori_loop(1, devices, send, 0)
-        span = row_in.at[phase, pl.ds(0, devices - 1)]
+
+        each_peer(send)
+        result = beside()
+        span = incoming.at[pl.ds(0, devices - 1)]
         pltpu.make_async_copy(span, span, row_recv.at[phase]).wait()
-        return jnp.sum(row_in[phase], axis=0)
+        return jnp.sum(incoming[...], axis=0), result
 
     def weight(row, at):
         return row[:, at : at + 1]
@@ -365,36 +405,101 @@
     image_parts = operate([tile_of(start, t) for t in range(tiles)], 0, greeted)
     for t in range(tiles):
         image[:, pl.ds(t * LANES, LANES)] = image_parts[t]
+    rows, listed = pair_rows(kept)
+    fresh = 2 * kept + 3
+
+    def gram():
+        partials = []
+        block = 4
+        for left in range(0, kept, block):
+            for right in range(left, kept, block):
+                wanted = [
+                    (one, two)
+                    for one in range(left, left + block)
+                    for two in range(max(right, one), right + block)
+                ]
+
+                def body(step, carry):
+                    base = pl.multiple_of(step * 8, 8)
+                    carry = list(carry)
+                    for tile in range(tiles):
+                        at = (pl.ds(base, 8), pl.ds(tile * LANES, LANES))
+                        ones = [basis[(left + m,) + at] for m in range(block)]
+                        twos = ones if left == right else [
+                            basis[(right + m,) + at] for m in range(block)
+                        ]
+                        for spot, (one, two) in enumerate(wanted):
+                            carry[spot] = carry[spot] + ones[one - left] * twos[two - right]
+                    return tuple(carry)
+
+                zero = jnp.zeros((8, LANES), jnp.float32)
+                partials += list(
+                    lax.fori_loop(0, elements // 8, body, (zero,) * len(wanted))
+                )
+        gram_rows = []
+        for begin in range(0, rows * LANES, LANES):
+            lo = max(begin, fresh)
+            here = partials[lo - fresh : begin + LANES - fresh]
+            row = to_row(here, lo - begin) if here else jnp.zeros((1, LANES), jnp.float32)
+            gram_rows.append(row)
+        return gram_rows
+
     row = to_row([folded(basis[at] * image[...]) for at in range(kept)])
-    proj_one = all_sum(row, 0) / total
+    sums, gram_part = all_sum(row, 0, gram)
+    proj_one = sums / total
     acc = image[...]
     for at in range(kept):
         acc = acc - weight(proj_one, at) * basis[at]
     first[...] = acc
 
+    with_first = []
+
+    def project_first():
+        with_first.extend(
+            [folded(basis[at] * first[...]) for at in range(kept)]
+            + [folded(first[...] * first[...])]
+        )
+
     image_parts = operate(
-        [first[:, pl.ds(t * LANES, LANES)] for t in range(tiles)], 1, lambda: None
+        [first[:, pl.ds(t * LANES, LANES)] for t in range(tiles)], 1, lambda: None, project_first
     )
     for t in range(tiles):
         image[:, pl.ds(t * LANES, LANES)] = image_parts[t]
     row = to_row(
         [folded(basis[at] * image[...]) for at in range(kept)]
-        + [folded(first[...] * first[...]), folded(first[...] * image[...])]
+        + [folded(first[...] * image[...]), folded(image[...] * image[...])]
+        + with_first
     )
-    sums = all_sum(row, 1) / total
-    norm_one = jnp.sqrt(weight(sums, kept) + epsilon)
+    block = jnp.concatenate([gram_part[0] + row] + gram_part[1:], axis=0)
+    sums, _ = all_sum(block, 1, lambda: None)
+    sums = sums / total
+    along = sums[0:1]
+    norm_one = jnp.sqrt(weight(along, fresh - 1) + epsilon)
     scale_one = 1.0 / norm_one
-    proj_two = sums * scale_one
-    self_two = weight(sums, kept + 1) * scale_one * scale_one
+    proj_two = along * scale_one
+    self_two = weight(along, kept) * scale_one * scale_one
+
+    spot = lax.broadcasted_iota(jnp.int32, (8, LANES), 1)
+    factor = jnp.broadcast_to(along, (8, LANES))
+    factor = jnp.where(spot < kept, -factor, 0.0)
+    factor = jnp.where(spot == kept, -self_two, factor)
+    factor = jnp.where(spot == kept + 1, 1.0, factor)
+    square = jnp.zeros((1, LANES), jnp.float32)
+    for at in range(rows):
+        left = jnp.broadcast_to(pairs[pl.ds(at, 1), :], (8, LANES))
+        right = jnp.broadcast_to(pairs[pl.ds(rows + at, 1), :], (8, LANES))
+        product = take_lanes(factor, left) * take_lanes(factor, right)
+        product = jnp.where(left == right, product, 2.0 * product)
+        used = spot + at * LANES < len(listed)
+        square = square + jnp.where(used, product * sums[at : at + 1], 0.0)[0:1]
+    square = jnp.maximum(jnp.sum(square, axis=1, keepdims=True), 0.0) * (scale_one * scale_one)
+    norm_two = jnp.sqrt(square + epsilon)
+
     acc = image[...] - (self_two * first[...])
     for at in range(kept):
-        acc = acc - weight(sums, at) * basis[at]
-    acc = acc * scale_one
+        acc = acc - weight(along, at) * basis[at]
     out[0] = first[...] * scale_one
-    image[...] = acc
-    square = all_sum(to_row([folded(acc * acc)]), 2) / total
-    norm_two = jnp.sqrt(weight(square, 0) + epsilon)
-    out[1] = image[...] * (1.0 / norm_two)
+    out[1] = acc * (scale_one / norm_two)
 
     spot = lax.broadcasted_iota(jnp.int32, (1, LANES), 1)
     row_first = jnp.where(spot < kept, proj_one, jnp.where(spot == kept, norm_one, 0.0))
@@ -409,8 +514,8 @@
             def _():
                 face_copy(step, side).wait_send()
 
-    for phase in range(3):
-        span = row_in.at[phase, pl.ds(0, devices - 1)]
+    for phase in range(2):
+        span = messages[phase][1].at[pl.ds(0, devices - 1)]
         pltpu.make_async_copy(span, span, row_send.at[phase]).wait()
 
 
@@ -419,21 +524,26 @@
     tiles = points // LANES
     devices = n_wide * n_narrow
     forward, backward, coef = tables()
+    rows, listed = pair_rows(kept)
+    pairs = np.zeros((2 * rows, LANES), np.int32)
+    for at, (left, right) in enumerate(listed):
+        pairs[at // LANES, at % LANES] = left
+        pairs[rows + at // LANES, at % LANES] = right
+    pairs = jnp.asarray(pairs)
     anywhere = pl.BlockSpec(memory_space=pl.ANY)
     vmem = pl.BlockSpec(memory_space=pltpu.VMEM)
     f32 = jnp.float32
     border = EX * EY
-    return pl.pallas_call(
+    shapes = ((2, elements, points), (2, kept + 2))
+    held = pl.pallas_call(
         functools.partial(kernel, n_wide, n_narrow),
-        out_shape=(
-            jax.ShapeDtypeStruct((2, elements, points), f32),
-            jax.ShapeDtypeStruct((2, kept + 2), f32),
-        ),
+        out_shape=tuple(pltpu.VMEM(shape, f32) for shape in shapes),
         in_specs=[
             pl.BlockSpec(memory_space=pltpu.SMEM),
             anywhere,
             anywhere,
             vmem,
+            anywhere,
             anywhere,
             anywhere,
             anywhere,
@@ -455,17 +565,21 @@
             pltpu.VMEM((elements, LANES), f32),
             pltpu.VMEM((2, 4, border, LANES), f32),
             pltpu.VMEM((2, 4, border, LANES), f32),
-            pltpu.VMEM((3, 1, LANES), f32),
-            pltpu.VMEM((3, devices, 1, LANES), f32),
-            pltpu.SemaphoreType.DMA((8,)),
+            pltpu.VMEM(pairs.shape, jnp.int32),
+            pltpu.VMEM((1, LANES), f32),
+            pltpu.VMEM((devices, 1, LANES), f32),
+            pltpu.VMEM((rows, LANES), f32),
+            pltpu.VMEM((devices, rows, LANES), f32),
+            pltpu.SemaphoreType.DMA((9,)),
             pltpu.SemaphoreType.DMA((2, 4)),
             pltpu.SemaphoreType.DMA((2, 4)),
-            pltpu.SemaphoreType.DMA((3,)),
-            pltpu.SemaphoreType.DMA((3,)),
+            pltpu.SemaphoreType.DMA((2,)),
+            pltpu.SemaphoreType.DMA((2,)),
         ],
         compiler_params=pltpu.CompilerParams(collective_id=0, has_side_effects=True),
         name="arnoldi",
-    )(restart_coeffs, old_basis, geometry, orientation, forward, backward, coef)
+    )(restart_coeffs, old_basis, geometry, orientation, forward, backward, coef, pairs)
+    return held
 
 
 def solution(mesh):

time: 34.5 us -> 27.4 us (0.79)
  Pallas kernels: 30.7 us -> 25.3 us
  local copies, waits for them, and re-layouts: 2.9 us -> 1.27 us
    pallas_call x1, Pallas kernels: 30.7 us -> 25.3 us  [on_device(): pl.pallas_call(functools.partial(kernel, n_wide, n_narrow), out_shape=tup...]
    unnamed x2, local copies, waits for them, and re-layouts: 2.9 us -> 1.27 us
where the time goes in v2:
time: 27.4 us; the launch traced here: 27.2 us
  Pallas kernels  25.3 us (92%)
  local copies, waits for them, and re-layouts  1.27 us (5%)
  between operations  0.64 us (2%)
    pallas_call x1, Pallas kernels, on_device(): pl.pallas_call(functools.partial(kernel, n_wide, n_narrow), out_shape=tup...  25.3 us
    unnamed x2, local copies, waits for them, and re-layouts  1.27 us

profile of v2, /device:TPU:0, one launch (start us, length us, event | category | flops | bytes accessed | tf_op | source)
XLA Modules:
  0.0 27.2 jit_solution(17571160766538743629)
XLA Ops:
  0.6 25.3 %arnoldi.1 = (f32[2,64,512]{2,1,0:T(8,128)S(1)}, f32[2,18]{1,0:T(2,128)S(1)}) custom-call(f32[16]{0:T(128)} %coeffs.1, f32[16,64,512]{2,1,0:T(8,128)} %basis_hbm.1, f32[4,64,512]{2,1,0:T(8,128)} %geom_hbm.1, s32[6,64]{1,0:T(8,128)} %orient.1, f32[128,256]{1,0:T(8,128)} %constant.8.clone.forward_hbm, f32[256,128]{1,0:T(8,128)} %constant.9.clone.backward_hbm, ...), custom_call_target="tpu_custom_call" | custom-call | tf_op jit(solution)/shard_map/arnoldi/pallas_call | solution.py:538
  25.9 0.7 %copy.12 = f32[2,64,512]{2,1,0:T(8,128)} copy(f32[2,64,512]{2,1,0:T(8,128)S(1)} %get-tuple-element.2) | data formatting | bytes 524288
  26.6 0.6 %copy.13 = f32[2,18]{1,0:T(2,128)} copy(f32[2,18]{1,0:T(2,128)S(1)} %get-tuple-element.3) | data formatting | bytes 288

commit v3 on v2

--- a/solution.py
+++ b/solution.py
@@ -291,21 +291,25 @@
 
     def operate(parts, step, ready, beside=lambda: None):
         result = local(parts)
+        def send_faces(sides):
+            for side in sides:
+
+                @pl.when(has[side])
+                def _():
+                    face_copy(step, side).start()
+
+        found_z = faces(result, pick_z)
+        face_z[...] = found_z
+        outbox[step, 2] = face_z[pl.ds(0, EX * EY, stride=EZ), :]
+        outbox[step, 3] = face_z[pl.ds(EZ - 1, EX * EY, stride=EZ), :]
+        ready()
+        send_faces((2, 3))
         found_y = faces(result, pick_y)
-        found_z = faces(result, pick_z)
         face_y[...] = found_y
-        face_z[...] = found_z
         for ex in range(EX):
             outbox[step, 0, pl.ds(ex * EZ, EZ), :] = face_y[pl.ds(ex * EY * EZ, EZ), :]
             outbox[step, 1, pl.ds(ex * EZ, EZ), :] = face_y[pl.ds(ex * EY * EZ + (EY - 1) * EZ, EZ), :]
-        outbox[step, 2] = face_z[pl.ds(0, EX * EY, stride=EZ), :]
-        outbox[step, 3] = face_z[pl.ds(EZ - 1, EX * EY, stride=EZ), :]
-        ready()
-        for side in (2, 3, 0, 1):
-
-            @pl.when(has[side])
-            def _():
-                face_copy(step, side).start()
+        send_faces((0, 1))
 
         face_x = jnp.where(low_half, result[0], result[tiles - 1])
         width = EY * EZ
@@ -327,24 +331,30 @@
 
         beside()
 
-        for side in range(4):
-
-            @pl.when(has[side])
-            def _():
-                face_arrival(step, side).wait()
-
+        def await_faces(sides):
+            for side in sides:
+
+                @pl.when(has[side])
+                def _():
+                    face_arrival(step, side).wait()
+
+        await_faces((0, 1))
         for ex in range(EX):
             halo_y[pl.ds(ex * EY * EZ, EZ), :] = inbox[step, 0, pl.ds(ex * EZ, EZ), :]
             halo_y[pl.ds(ex * EY * EZ + (EY - 1) * EZ, EZ), :] = inbox[step, 1, pl.ds(ex * EZ, EZ), :]
+        edge_y = row_y == jnp.where(low_half, EY - 1, 0)
+        in_y = jnp.where(edge_y, halo_y[...], in_y)
+        for t in range(tiles):
+            result[t] = result[t] + jnp.where(at_y, take_lanes(in_y, index[t]), 0.0)
+            image[:, pl.ds(t * LANES, LANES)] = result[t]
+
+        await_faces((2, 3))
         halo_z[pl.ds(0, EX * EY, stride=EZ), :] = inbox[step, 2]
         halo_z[pl.ds(EZ - 1, EX * EY, stride=EZ), :] = inbox[step, 3]
-        edge_y = row_y == jnp.where(low_half, EY - 1, 0)
         edge_z = row_z == jnp.where(low_half, EZ - 1, 0)
-        in_y = jnp.where(edge_y, halo_y[...], in_y)
         in_z = jnp.where(edge_z, halo_z[...], in_z)
         return [
-            result[t]
-            + jnp.where(at_y, take_lanes(in_y, index[t]), 0.0)
+            image[:, pl.ds(t * LANES, LANES)]
             + jnp.where(at_z, take_lanes(in_z, index[tiles + t]), 0.0)
             for t in range(tiles)
         ]

time: 27.4 us -> 27.1 us (0.989)
  Pallas kernels: 25.3 us -> 25 us
where the time goes in v3:
time: 27.1 us; the launch traced here: 26.9 us
  Pallas kernels  25 us (92%)
  local copies, waits for them, and re-layouts  1.27 us (5%)
  between operations  0.64 us (2%)
    pallas_call x1, Pallas kernels, on_device(): pl.pallas_call(functools.partial(kernel, n_wide, n_narrow), out_shape=tup...  25 us
    unnamed x2, local copies, waits for them, and re-layouts  1.27 us

profile of v3, /device:TPU:0, one launch (start us, length us, event | category | flops | bytes accessed | tf_op | source)
XLA Modules:
  0.0 26.9 jit_solution(15466774315187194281)
XLA Ops:
  0.6 25.0 %arnoldi.1 = (f32[2,64,512]{2,1,0:T(8,128)S(1)}, f32[2,18]{1,0:T(2,128)S(1)}) custom-call(f32[16]{0:T(128)} %coeffs.1, f32[16,64,512]{2,1,0:T(8,128)} %basis_hbm.1, f32[4,64,512]{2,1,0:T(8,128)} %geom_hbm.1, s32[6,64]{1,0:T(8,128)} %orient.1, f32[128,256]{1,0:T(8,128)} %constant.8.clone.forward_hbm, f32[256,128]{1,0:T(8,128)} %constant.9.clone.backward_hbm, ...), custom_call_target="tpu_custom_call" | custom-call | tf_op jit(solution)/shard_map/arnoldi/pallas_call | solution.py:548
  25.7 0.7 %copy.12 = f32[2,64,512]{2,1,0:T(8,128)} copy(f32[2,64,512]{2,1,0:T(8,128)S(1)} %get-tuple-element.2) | data formatting | bytes 524288
  26.4 0.6 %copy.13 = f32[2,18]{1,0:T(2,128)} copy(f32[2,18]{1,0:T(2,128)S(1)} %get-tuple-element.3) | data formatting | bytes 288
